TPU v7x, 32 devices: a whole 2x2x4 slice. The times are simulated.
32 devices in a mesh: batch: 2 (over x), col: 4 (over z), row: 4 (over y, core).
Axes of the slice: x: 2, y: 2, z: 4, core: 2. Of those that a mesh axis runs over, the one named last changes fastest.
Arguments:
- d_inv: bfloat16 [384, 256, 256], P(('batch', 'row')), parts along dimension 0
- l_blk: bfloat16 [384, 256, 256], P(('batch', 'row')), parts along dimension 0
- u_blk: bfloat16 [384, 256, 256], P(('batch', 'row')), parts along dimension 0
- rhs_blk: float32 [384, 256, 512], P(('batch', 'row'), None, 'col'), parts along dimension 0
- x_init: float32 [384, 256, 512], P(('batch', 'row'), None, 'col'), parts along dimension 0
Outputs:
- output: float32 [384, 256, 512], P(('batch', 'row'), None, 'col'), parts along dimension 0
There are 2 independent parts. A program takes and returns all parts, laid end to end along the dimension named above; each array names one.
All inputs are finite; a program needn't handle non-finite values.
Results may differ from a plain program's by a relative error of at most 0.0117393.
Values are sent between devices in bfloat16 or wider.
A program may use at most 1 GiB of HBM per device.

v0:
```python
import jax
import jax.numpy as jnp
from jax import lax
from jax.sharding import PartitionSpec as P

SWEEPS = 4


def row_step(x_left, row_in):
    d_i, l_i, u_i, f_i, x_right = row_in
    t_i = (f_i
           - jnp.dot(l_i, x_left.astype(jnp.bfloat16), preferred_element_type=jnp.float32)
           - jnp.dot(u_i, x_right.astype(jnp.bfloat16), preferred_element_type=jnp.float32))
    x_i = jnp.dot(d_i, t_i.astype(jnp.bfloat16), preferred_element_type=jnp.float32)
    return x_i, x_i


def solution(mesh):
    chain_len = mesh.shape["row"]
    mat_spec = P(("batch", "row"), None, None)
    vec_spec = P(("batch", "row"), None, "col")
    fwd_perm = [(src_dev, src_dev + 1) for src_dev in range(chain_len - 1)]
    back_perm = [(src_dev + 1, src_dev) for src_dev in range(chain_len - 1)]

    def device_fn(d_inv, l_blk, u_blk, rhs_blk, x_init):
        chain_pos = lax.axis_index("row")
        zero_blk = jnp.zeros(x_init.shape[1:], jnp.float32)
        x_cur = x_init
        for sweep_idx in range(SWEEPS):
            from_right = lax.ppermute(x_cur[0], "row", back_perm)
            x_right = jnp.concatenate([x_cur[1:], from_right[None]], axis=0)

            def local_sweep(x_left, x_right=x_right):
                _, x_new = lax.scan(row_step, x_left, (d_inv, l_blk, u_blk, rhs_blk, x_right))
                return x_new

            def run_stage(stage_idx, stage_state, local_sweep=local_sweep):
                x_run, x_left = stage_state
                x_run = lax.cond(chain_pos == stage_idx, lambda: local_sweep(x_left), lambda: x_run)
                x_left = lax.ppermute(x_run[-1], "row", fwd_perm)
                return x_run, x_left

            x_cur, _ = lax.fori_loop(0, chain_len, run_stage, (x_cur, zero_blk))
        return x_cur

    return jax.shard_map(device_fn, mesh=mesh, in_specs=(mat_spec, mat_spec, mat_spec, vec_spec, vec_spec), out_specs=vec_spec, check_vma=False)
```

profile of v0, /device:TPU:31, one launch (start us, length us, event | category | flops | bytes accessed | tf_op | source)
XLA Modules:
  0.0 2069.6 jit_solution(12593508579084171643)
XLA Ops:
  0.0 2.8 copy.100
  2.8 2.6 collective-permute-start.4
  8.2 622.7 %while.120 = (s32[]{:T(128)}, f32[48,256,128]{2,1,0:T(8,128)}, bf16[256,128]{1,0:T(8,128)(2,1)S(1)}, s32[]{:T(128)}, bf16[48,256,256]{2,1,0:T(8,128)(2,1)}, /*in...) while((s32[]{:T(128)}, f32[48,256,128]{2,1,0:T(8,128)}, ...), condition=%wide.region_5.6_spmd, body=%wide.region_0.5_spmd.sunk | while | flops 50462724 | bytes 1510784 | solution.py:43
  10.4 2.4 collective-permute-done.3
  15.0 4.3 collective-permute-done.3
  21.5 453.7 %collective-permute-done.3 = bf16[256,128]{1,0:T(8,128)(2,1)S(1)} collective-permute-done((bf16[256,128]{1,0:T(8,128)(2,1)S(1)}, bf16[256,128]{1,0:T(8,128)(2,1)S(1)}, u32[]{:S(2)}, u32[]{:S(2)}) %collective-permute-start.3) | collective-permute-done | bytes 65568 | tf_op jit(solution)/shard_map/while/body/eval_jaxpr/ppermute | solution.py:40
  475.3 151.6 %conditional.8 = (f32[48,256,128]{2,1,0:T(8,128)}) conditional(s32[]{:T(128)} %convert_element_type.132, f32[48,256,128]{2,1,0:T(8,128)} %get-tuple-element.1600, (bf16[48,256,256]{2,1,0:T(8,128)(2,1)}, f32[48,256,128]{2,1,0:T(8,128)}, bf16[48,256,256]{2,1,0:T(8,128)(2,1)}, bf16[48,256,256]{2,1,0:T(8,128)(2,1)}, bf16[48,256,128]{2,1,0:T(8,128)(2,1)}, ...), branch_computations={%region_1.0_spmd, %region_2.4_spmd} | conditional | flops 50462720 | bytes 1117365 | solution.py:39
  475.3 151.6 %while.116 = (s32[]{:T(128)}, bf16[256,128]{1,0:T(8,128)(2,1)S(1)}, f32[48,256,128]{2,1,0:T(8,128)}, bf16[48,256,256]{2,1,0:T(8,128)(2,1)}, f32[48,256,128]{2,1,...) while((s32[]{:T(128)}, bf16[256,128]{1,0:T(8,128)(2,1)S(1)}, ...), condition=%wide.region_4.3_spmd, body=%wide.region_3.2_spmd.sunk | while | flops 50462720 | bytes 1117277 | solution.py:34
  631.8 2.1 collective-permute-start.5
  633.9 3.2 slice.54
  637.4 473.0 %while.121 = (s32[]{:T(128)}, f32[48,256,128]{2,1,0:T(8,128)}, bf16[256,128]{1,0:T(8,128)(2,1)S(1)}, s32[]{:T(128)}, bf16[48,256,256]{2,1,0:T(8,128)(2,1)}, /*in...) while((s32[]{:T(128)}, f32[48,256,128]{2,1,0:T(8,128)}, ...), condition=%wide.region_11.12_spmd, body=%wide.region_6.11_spmd.sunk | while | flops 50462724 | bytes 1510784 | solution.py:43
  643.7 3.8 collective-permute-done.2
  649.7 305.1 %collective-permute-done.2 = bf16[256,128]{1,0:T(8,128)(2,1)S(1)} collective-permute-done((bf16[256,128]{1,0:T(8,128)(2,1)S(1)}, bf16[256,128]{1,0:T(8,128)(2,1)S(1)}, u32[]{:S(2)}, u32[]{:S(2)}) %collective-permute-start.2) | collective-permute-done | bytes 65568 | tf_op jit(solution)/shard_map/while/body/eval_jaxpr/ppermute | solution.py:40
  954.8 151.6 %conditional.9 = (f32[48,256,128]{2,1,0:T(8,128)}) conditional(s32[]{:T(128)} %convert_element_type.133, f32[48,256,128]{2,1,0:T(8,128)} %get-tuple-element.1630, (bf16[48,256,256]{2,1,0:T(8,128)(2,1)}, f32[48,256,128]{2,1,0:T(8,128)}, bf16[48,256,256]{2,1,0:T(8,128)(2,1)}, bf16[48,256,256]{2,1,0:T(8,128)(2,1)}, bf16[48,256,128]{2,1,0:T(8,128)(2,1)S(1)}, ...), branch_computations={%region_7.7_spmd, %region_8.10_spmd} | conditional | flops 50462720 | bytes 1117365 | solution.py:39
  954.8 151.6 %while.117 = (s32[]{:T(128)}, bf16[256,128]{1,0:T(8,128)(2,1)S(1)}, f32[48,256,128]{2,1,0:T(8,128)}, bf16[48,256,256]{2,1,0:T(8,128)(2,1)}, f32[48,256,128]{2,1,...) while((s32[]{:T(128)}, bf16[256,128]{1,0:T(8,128)(2,1)S(1)}, ...), condition=%wide.region_10.9_spmd, body=%wide.region_9.8_spmd.sunk | while | flops 50462720 | bytes 1117277 | solution.py:34
  959.1 2.0 bitcast_dynamic-update-slice_fusion.10
  962.3 2.0 bitcast_dynamic-update-slice_fusion.10
  965.5 2.0 bitcast_dynamic-update-slice_fusion.10
  968.6 2.0 bitcast_dynamic-update-slice_fusion.10
  971.8 2.0 bitcast_dynamic-update-slice_fusion.10
  974.9 2.0 bitcast_dynamic-update-slice_fusion.10
  978.1 2.0 bitcast_dynamic-update-slice_fusion.10
  981.2 2.0 bitcast_dynamic-update-slice_fusion.10
  984.4 2.0 bitcast_dynamic-update-slice_fusion.10
  987.6 2.0 bitcast_dynamic-update-slice_fusion.10
  990.7 2.0 bitcast_dynamic-update-slice_fusion.10
  993.9 2.0 bitcast_dynamic-update-slice_fusion.10
  997.0 2.0 bitcast_dynamic-update-slice_fusion.10
  1000.2 2.0 bitcast_dynamic-update-slice_fusion.10
  1003.3 2.0 bitcast_dynamic-update-slice_fusion.10
  1006.5 2.0 bitcast_dynamic-update-slice_fusion.10
  1009.7 2.0 bitcast_dynamic-update-slice_fusion.10
  1012.8 2.0 bitcast_dynamic-update-slice_fusion.10
  1016.0 2.0 bitcast_dynamic-update-slice_fusion.10
  1019.1 2.0 bitcast_dynamic-update-slice_fusion.10
  1022.3 2.0 bitcast_dynamic-update-slice_fusion.10
  1025.5 2.0 bitcast_dynamic-update-slice_fusion.10
  1028.6 2.0 bitcast_dynamic-update-slice_fusion.10
  1031.8 2.0 bitcast_dynamic-update-slice_fusion.10
  1034.9 2.0 bitcast_dynamic-update-slice_fusion.10
  1038.1 2.0 bitcast_dynamic-update-slice_fusion.10
  1041.2 2.0 bitcast_dynamic-update-slice_fusion.10
  1044.4 2.0 bitcast_dynamic-update-slice_fusion.10
  1047.6 2.0 bitcast_dynamic-update-slice_fusion.10
  1082.3 2.0 bitcast_dynamic-update-slice_fusion.10
  1111.4 2.1 collective-permute-start.6
  1113.4 3.2 slice.56
  1117.0 473.0 %while.122 = (s32[]{:T(128)}, f32[48,256,128]{2,1,0:T(8,128)}, bf16[256,128]{1,0:T(8,128)(2,1)S(1)}, s32[]{:T(128)}, bf16[48,256,256]{2,1,0:T(8,128)(2,1)}, /*in...) while((s32[]{:T(128)}, f32[48,256,128]{2,1,0:T(8,128)}, ...), condition=%wide.region_17.18_spmd, body=%wide.region_12.17_spmd.sunk | while | flops 50462724 | bytes 1510784 | solution.py:43
  1123.3 3.8 collective-permute-done.1
  1129.3 305.1 %collective-permute-done.1 = bf16[256,128]{1,0:T(8,128)(2,1)S(1)} collective-permute-done((bf16[256,128]{1,0:T(8,128)(2,1)S(1)}, bf16[256,128]{1,0:T(8,128)(2,1)S(1)}, u32[]{:S(2)}, u32[]{:S(2)}) %collective-permute-start.1) | collective-permute-done | bytes 65568 | tf_op jit(solution)/shard_map/while/body/eval_jaxpr/ppermute | solution.py:40
  1434.4 151.6 %conditional.10 = (f32[48,256,128]{2,1,0:T(8,128)}) conditional(s32[]{:T(128)} %convert_element_type.134, f32[48,256,128]{2,1,0:T(8,128)} %get-tuple-element.1660, (bf16[48,256,256]{2,1,0:T(8,128)(2,1)}, f32[48,256,128]{2,1,0:T(8,128)}, bf16[48,256,256]{2,1,0:T(8,128)(2,1)}, bf16[48,256,256]{2,1,0:T(8,128)(2,1)}, ...), branch_computations={%region_13.13_spmd, %region_14.16_spmd} | conditional | flops 50462720 | bytes 1117365 | solution.py:39
  1434.4 151.6 %while.118 = (s32[]{:T(128)}, bf16[256,128]{1,0:T(8,128)(2,1)S(1)}, f32[48,256,128]{2,1,0:T(8,128)}, bf16[48,256,256]{2,1,0:T(8,128)(2,1)}, f32[48,256,128]{2,1,...) while((s32[]{:T(128)}, bf16[256,128]{1,0:T(8,128)(2,1)S(1)}, ...), condition=%wide.region_16.15_spmd, body=%wide.region_15.14_spmd.sunk | while | flops 50462720 | bytes 1117277 | solution.py:34
  1470.3 2.0 bitcast_dynamic-update-slice_fusion.9
  1530.3 2.0 bitcast_dynamic-update-slice_fusion.9
  1591.0 2.1 collective-permute-start.7
  1593.0 3.2 slice.58
  1596.6 473.0 %while.123 = (s32[]{:T(128)}, f32[48,256,128]{2,1,0:T(8,128)}, bf16[256,128]{1,0:T(8,128)(2,1)S(1)}, s32[]{:T(128)}, bf16[48,256,256]{2,1,0:T(8,128)(2,1)}, /*in...) while((s32[]{:T(128)}, f32[48,256,128]{2,1,0:T(8,128)}, ...), condition=%wide.region_23.24_spmd, body=%wide.region_18.23_spmd.sunk | while | flops 50462724 | bytes 1510784 | solution.py:43
  1602.9 3.8 collective-permute-done
  1608.9 305.1 %collective-permute-done = bf16[256,128]{1,0:T(8,128)(2,1)S(1)} collective-permute-done((bf16[256,128]{1,0:T(8,128)(2,1)S(1)}, bf16[256,128]{1,0:T(8,128)(2,1)S(1)}, u32[]{:S(2)}, u32[]{:S(2)}) %collective-permute-start) | collective-permute-done | bytes 65568 | tf_op jit(solution)/shard_map/while/body/eval_jaxpr/ppermute | solution.py:40
  1914.0 151.6 %conditional.11 = (f32[48,256,128]{2,1,0:T(8,128)}) conditional(s32[]{:T(128)} %convert_element_type.135, f32[48,256,128]{2,1,0:T(8,128)} %get-tuple-element.1690, (bf16[48,256,256]{2,1,0:T(8,128)(2,1)}, f32[48,256,128]{2,1,0:T(8,128)}, bf16[48,256,256]{2,1,0:T(8,128)(2,1)}, bf16[48,256,256]{2,1,0:T(8,128)(2,1)}, ...), branch_computations={%region_19.19_spmd, %region_20.22_spmd} | conditional | flops 50462720 | bytes 1117365 | solution.py:39
  1914.0 151.6 %while.119 = (s32[]{:T(128)}, bf16[256,128]{1,0:T(8,128)(2,1)S(1)}, f32[48,256,128]{2,1,0:T(8,128)}, bf16[48,256,256]{2,1,0:T(8,128)(2,1)}, f32[48,256,128]{2,1,...) while((s32[]{:T(128)}, bf16[256,128]{1,0:T(8,128)(2,1)S(1)}, ...), condition=%wide.region_22.21_spmd, body=%wide.region_21.20_spmd.sunk | while | flops 50462720 | bytes 1117277 | solution.py:34
  1918.3 2.0 bitcast_dynamic-update-slice_fusion.8
  1978.3 2.0 bitcast_dynamic-update-slice_fusion.8
  2038.3 2.0 bitcast_dynamic-update-slice_fusion.8
  (423 shorter events, 588.6 us)
Async XLA Ops:
  2.8 2.7 copy-start
  2.8 3.5 collective-permute-start.4
  9.1 3.7 collective-permute-start.3
  13.7 5.6 collective-permute-start.3
  20.3 455.0 %collective-permute-start.3 = (bf16[256,128]{1,0:T(8,128)(2,1)S(1)}, bf16[256,128]{1,0:T(8,128)(2,1)S(1)}, u32[]{:S(2)}, u32[]{:S(2)}) collective-permute-start(bf16[256,128]{1,0:T(8,128)(2,1)S(1)} %slice_bitcast_fusion.12), channel_id=1, source_target_pairs={{0,1},{1,2},{2,3},{4,5},{5,6},{6,7},{8,9},{9,10},{10,11},{12,13},{... | collective-permute-start | bytes 196616 | tf_op jit(solution)/shard_map/while/body/eval_jaxpr/ppermute | solution.py:40
  627.8 3.1 collective-permute-start.3
  631.8 5.3 collective-permute-start.5
  638.4 3.1 collective-permute-start.2
  642.4 5.1 collective-permute-start.2
  648.4 306.4 %collective-permute-start.2 = (bf16[256,128]{1,0:T(8,128)(2,1)S(1)}, bf16[256,128]{1,0:T(8,128)(2,1)S(1)}, u32[]{:S(2)}, u32[]{:S(2)}) collective-permute-start(bf16[256,128]{1,0:T(8,128)(2,1)S(1)} %slice_bitcast_fusion.13), channel_id=1, source_target_pairs={{0,1},{1,2},{2,3},{4,5},{5,6},{6,7},{8,9},{9,10},{10,11},{12,13},{... | collective-permute-start | bytes 196616 | tf_op jit(solution)/shard_map/while/body/eval_jaxpr/ppermute | solution.py:40
  1107.3 3.1 collective-permute-start.2
  1111.4 5.3 collective-permute-start.6
  1118.0 3.1 collective-permute-start.1
  1122.0 5.1 collective-permute-start.1
  1128.0 306.4 %collective-permute-start.1 = (bf16[256,128]{1,0:T(8,128)(2,1)S(1)}, bf16[256,128]{1,0:T(8,128)(2,1)S(1)}, u32[]{:S(2)}, u32[]{:S(2)}) collective-permute-start(bf16[256,128]{1,0:T(8,128)(2,1)S(1)} %slice_bitcast_fusion.14), channel_id=1, source_target_pairs={{0,1},{1,2},{2,3},{4,5},{5,6},{6,7},{8,9},{9,10},{10,11},{12,13},{... | collective-permute-start | bytes 196616 | tf_op jit(solution)/shard_map/while/body/eval_jaxpr/ppermute | solution.py:40
  1586.9 3.1 collective-permute-start.1
  1591.0 5.3 collective-permute-start.7
  1597.5 3.1 collective-permute-start
  1601.6 5.1 collective-permute-start
  1607.6 306.4 %collective-permute-start = (bf16[256,128]{1,0:T(8,128)(2,1)S(1)}, bf16[256,128]{1,0:T(8,128)(2,1)S(1)}, u32[]{:S(2)}, u32[]{:S(2)}) collective-permute-start(bf16[256,128]{1,0:T(8,128)(2,1)S(1)} %slice_bitcast_fusion.15), channel_id=1, source_target_pairs={{0,1},{1,2},{2,3},{4,5},{5,6},{6,7},{8,9},{9,10},{10,11},{12,13},{... | collective-permute-start | bytes 196616 | tf_op jit(solution)/shard_map/while/body/eval_jaxpr/ppermute | solution.py:40
  2066.5 3.1 collective-permute-start
where the time goes:
time: 2080 us; the launch traced here: 2070 us
  waiting for transfers between devices  1400 us (67%)
  matrix products  605 us (29%)
  local copies, waits for them, and re-layouts  30.5 us (1%)
  starting transfers between devices  29.2 us (1%)
    ppermute x16, waiting for transfers between devices, run_stage(): x_left = lax.ppermute(x_run[-1], 'row', fwd_perm)  1400 us
    dot_general x192, matrix products, row_step(): jnp.dot(d_i, t_i.astype(jnp.bfloat16), preferred_element_type=jnp.float32)  387 us
    dot_general x192, matrix products, row_step(): jnp.dot(l_i, x_left.astype(jnp.bfloat16), preferred_element_type=jnp.floa...  217 us
  transfers between devices with their start and end apart: 20, of which 17 were waited for; matrix products, arithmetic and copies ran while one was open for 0% of the time, Pallas kernels for 0%

commit v1 on v0

v1 whole, which is shorter than its diff:
```python
import jax
import jax.numpy as jnp
from jax import lax
from jax.experimental import pallas as pl
from jax.experimental.pallas import tpu as pltpu
from jax.sharding import PartitionSpec as P

SWEEPS = 4
GHOST = SWEEPS - 1
LEAD = 2 * SWEEPS - 1
UNROLL = 10
RING = 10
MESH = pl.DeviceIdType.MESH
ORDER = (1, 2, 3, 4)
BF16, F32 = jnp.bfloat16, jnp.float32


def n_ok(name, ring):
    return ring or name != "x"


def dot(a, b):
    return jnp.dot(a, b, preferred_element_type=F32)


def make_kernel(n_dev, n_rows, cols):
    last_row = n_rows - 1
    trips = (n_rows - LEAD - 1) // UNROLL
    main_end = LEAD + trips * UNROLL
    end = n_rows + LEAD
    first = LEAD + 1
    chunks = [(0, 1), (1, 1), (2, 2), (4, first - 4)]
    m0 = len(chunks)
    chunks += [(first + UNROLL * b, UNROLL) for b in range(trips)]
    assert first + UNROLL * trips == n_rows and UNROLL % RING == 0
    ghost = len(chunks)

    def kernel(d_hbm, l_hbm, u_hbm, f_hbm, x_hbm, o_hbm,
               l_all, d_all, u_all, f_raw, x_raw, f_all, x_all, l_ring, d_ring, u_ring, f_ring, out, now, recv, send,
               sem_l, sem_d, sem_u, sem_f, sem_x, sem_o, sem_g, sem_s, sem_r):
        me = lax.axis_index("row")
        arrays = {"l": (l_hbm, l_all, sem_l), "d": (d_hbm, d_all, sem_d), "u": (u_hbm, u_all, sem_u),
                  "f": (f_hbm, f_raw, sem_f), "x": (x_hbm, x_raw, sem_x)}

        def chunk(name, c, start=None, size=None):
            hbm, vmem, sem = arrays[name]
            if start is None:
                start, size = chunks[c]
            rows = pl.ds(start, size)
            return pltpu.make_async_copy(hbm.at[rows], vmem.at[rows], sem.at[c])

        for c in range(ghost):
            for name in "uxdfl":
                chunk(name, c).start()

        def ghost_rows(name):
            return GHOST + 1 if name == "x" else GHOST

        def ghost_copy(i, name):
            hbm, vmem, sem = arrays[name]
            n = ghost_rows(name)
            return pltpu.make_async_remote_copy(
                src_ref=hbm.at[pl.ds(0, n)], dst_ref=vmem.at[pl.ds(n_rows, n)], send_sem=sem_g.at[i],
                recv_sem=sem.at[ghost], device_id={"row": me - 1}, device_id_type=MESH)

        def ghost_local(name):
            hbm, vmem, sem = arrays[name]
            n = ghost_rows(name)
            return pltpu.make_async_copy(hbm.at[pl.ds(0, n)], vmem.at[pl.ds(n_rows, n)], sem.at[ghost])

        def ghost_wait(name):
            ghost_local(name).wait()

        barrier = pltpu.get_barrier_semaphore()

        @pl.when(me > 0)
        def _():
            pl.semaphore_signal(barrier, inc=1, device_id={"row": me - 1}, device_id_type=MESH)

        @pl.when(me < n_dev - 1)
        def _():
            pl.semaphore_signal(barrier, inc=1, device_id={"row": me + 1}, device_id_type=MESH)

        pl.semaphore_wait(barrier, jnp.where(me > 0, 1, 0) + jnp.where(me < n_dev - 1, 1, 0))

        @pl.when(me > 0)
        def _():
            for i, name in enumerate("xuldf"):
                ghost_copy(i, name).start()

        @pl.when(me == n_dev - 1)
        def _():
            for name in "xuldf":
                ghost_local(name).start()

        def boundary(k):
            return pltpu.make_async_remote_copy(
                src_ref=send.at[k], dst_ref=recv.at[k], send_sem=sem_s.at[k], recv_sem=sem_r.at[k],
                device_id={"row": me + 1}, device_id_type=MESH)

        def out_copy(i, start, size):
            rows = pl.ds(start, size)
            return pltpu.make_async_copy(out.at[rows], o_hbm.at[rows], sem_o.at[i])

        def run(ring):
            def where(base, p):
                return p if base is None else base + (p - LEAD)

            def slot(base, r):
                return r % RING if ring else where(base, r)

            big = {"l": l_all, "d": d_all, "u": u_all}
            prep_to = {"l": l_ring, "d": d_ring, "u": u_ring, "f": f_ring} if ring else dict(big, f=f_all)

            def prep(name, base, r):
                at = where(base, r)
                if name == "x":
                    x_all[at] = x_raw[at].astype(BF16).T
                elif name == "f":
                    prep_to["f"][slot(base, r)] = f_raw[at].T
                else:
                    prep_to[name][slot(base, r)] = big[name][at].T

            def active(k, s):
                return 0 <= s - 2 * (k - 1) <= last_row + SWEEPS - k

            def mat(name, base, r):
                return prep_to[name][slot(base, r)]

            def period(x, p, base=None):
                x = dict(x)
                if base is None and p % 2 == 0 and p < 2 * SWEEPS and not ring:
                    k = p // 2 + 1
                    boundary(k - 1).wait_recv()
                    x[k] = recv[k - 1]
                new = {}
                for k in ORDER:
                    if not active(k, p):
                        continue
                    r = p - 2 * (k - 1)
                    if k == 1:
                        right = x_all[where(base, r + 1)]
                    else:
                        right = x[k - 1]
                        if base is None and r == last_row:
                            right = jnp.where(me < n_dev - 1, right, jnp.zeros_like(right))
                    s = dot(right, mat("u", base, r))
                    if k in x:
                        s = s + dot(x[k], mat("l", base, r))
                    t = (prep_to["f"][slot(base, r)] - s).astype(BF16)
                    val = dot(t, mat("d", base, r))
                    new[k] = val.astype(BF16)
                    if k == SWEEPS:
                        out[where(base, r)] = val.T
                    if base is None and r == last_row:
                        send[k - 1] = new[k]

                        @pl.when(me < n_dev - 1)
                        def _():
                            boundary(k - 1).start()
                return new

            def step_preps(p):
                return [(n, p + 1) for n in "ldf"] + [("u", p + 2), ("x", p + 3)]

            waited = set()

            def need(name, r):
                c = max(i for i, (start, _) in enumerate(chunks) if start <= r)
                if (name, c) not in waited:
                    waited.add((name, c))
                    chunk(name, c).wait()

            if ring:
                waited.add(("x", 0))
                chunk("x", 0).wait()
                chunk("l", 0).wait()
                waited.add(("l", 0))
                for name, r in (("u", 0), ("x", 1), ("d", 0), ("f", 0), ("u", 1), ("x", 2)):
                    need(name, r)
                    prep(name, None, r)
            else:
                for c in range(m0):
                    for name in "uxdfl":
                        chunk(name, c).wait()
                for r in range(first):
                    for name in "uxdfl":
                        prep(name, None, r)

                def prepare(b, carry):
                    start = first + UNROLL * b
                    for name in "uxdfl":
                        chunk(name, m0 + b, start, UNROLL).wait()

                    def pair(i, carry):
                        for j in range(2):
                            for name in "uxdfl":
                                prep(name, start + 2 * i, LEAD + j)
                        return carry
                    return lax.fori_loop(0, UNROLL // 2, pair, carry)
                lax.fori_loop(0, trips, prepare, 0)
                ghost_wait("x")
                for r in range(n_rows, n_rows + GHOST + 1):
                    prep("x", None, r)

            def keep(x):
                for k in x:
                    now[k - 1] = x[k]

            def load():
                return {k: now[k - 1] for k in range(1, SWEEPS + 1)}

            x = {}
            for p in range(LEAD):
                for name, r in step_preps(p) if ring else ():
                    need(name, r)
                    prep(name, None, r)
                x = period(x, p)
            keep(x)
            out_copy(trips + 2, 0, 1).start()

            def trip(b, carry):
                base = LEAD + UNROLL * b
                if ring:
                    for name in "ldf":
                        chunk(name, m0 + b, first + UNROLL * b, UNROLL).wait()

                    @pl.when(b < trips - 1)
                    def _():
                        for name in "ux":
                            chunk(name, m0 + b + 1, first + UNROLL * (b + 1), UNROLL).wait()

                    @pl.when(b == trips - 1)
                    def _():
                        for name in "ux":
                            ghost_wait(name)
                x = load()
                for j in range(UNROLL):
                    p = LEAD + j
                    for name, r in step_preps(p) if ring else ():
                        prep(name, base, r)
                    x = period(x, p, base)
                keep(x)
                out_copy(b, 1 + UNROLL * b, UNROLL).start()
                return carry
            lax.fori_loop(0, trips, trip, 0)

            for name in "ldf" if ring else "uldf":
                ghost_wait(name)
            if not ring:
                prep("u", None, n_rows)
            x = load()
            for p in range(main_end, end - 1):
                for name, r in step_preps(p):
                    if n_rows <= r < n_rows + GHOST and (n_ok(name, ring)) or (ring and name == "x" and r == n_rows + GHOST):
                        prep(name, None, r)
                x = {**x, **period(x, p)}
                if p == end - 3:
                    out_copy(trips, 1 + UNROLL * trips, n_rows - UNROLL * trips - 2).start()
            out_copy(trips + 1, last_row, 1).start()

        @pl.when(me == 0)
        def _():
            run(True)

        @pl.when(me > 0)
        def _():
            run(False)

        @pl.when(me < n_dev - 1)
        def _():
            for k in range(SWEEPS):
                boundary(k).wait_send()

        @pl.when(me > 0)
        def _():
            for i, name in enumerate("xuldf"):
                ghost_copy(i, name).wait_send()
        for b in range(trips):
            out_copy(b, 1 + UNROLL * b, UNROLL).wait()
        out_copy(trips, 1 + UNROLL * trips, n_rows - UNROLL * trips - 2).wait()
        out_copy(trips + 2, 0, 1).wait()
        out_copy(trips + 1, last_row, 1).wait()

    def call(d_inv, l_blk, u_blk, rhs_blk, x_init):
        size = d_inv.shape[-1]
        ext = n_rows + GHOST
        dma = pltpu.SemaphoreType.DMA
        mat = lambda n: pltpu.VMEM((n, size, size), BF16)
        vec_t = lambda n, t: pltpu.VMEM((n, cols, size), t)
        vec = lambda n: pltpu.VMEM((n, size, cols), F32)
        return pl.pallas_call(
            kernel,
            out_shape=jax.ShapeDtypeStruct((n_rows, size, cols), F32),
            in_specs=[pl.BlockSpec(memory_space=pltpu.HBM)] * 5,
            out_specs=pl.BlockSpec(memory_space=pltpu.HBM),
            scratch_shapes=[
                mat(ext), mat(ext), mat(ext), vec(ext), vec(ext + 1), vec_t(ext, F32), vec_t(ext + 1, BF16),
                mat(RING), mat(RING), mat(RING), vec_t(RING, F32),
                vec(n_rows), vec_t(SWEEPS, BF16), vec_t(SWEEPS, BF16), vec_t(SWEEPS, BF16),
                *[dma((ghost + 1,)) for _ in range(5)], dma((trips + 3,)), dma((5,)), dma((SWEEPS,)), dma((SWEEPS,)),
            ],
            compiler_params=pltpu.CompilerParams(
                collective_id=0, has_side_effects=True, vmem_limit_bytes=67_000_000),
        )(d_inv, l_blk, u_blk, rhs_blk, x_init)

    return call


def solution(mesh):
    mat_spec = P(("batch", "row"), None, None)
    vec_spec = P(("batch", "row"), None, "col")
    n_dev = mesh.shape["row"]

    def device_fn(d_inv, l_blk, u_blk, rhs_blk, x_init):
        return make_kernel(n_dev, rhs_blk.shape[0], rhs_blk.shape[2])(d_inv, l_blk, u_blk, rhs_blk, x_init)

    return jax.shard_map(device_fn, mesh=mesh, in_specs=(mat_spec, mat_spec, mat_spec, vec_spec, vec_spec), out_specs=vec_spec, check_vma=False)
```

time: 2080 us -> 166 us (0.08)
  waiting for transfers between devices: 1400 us -> 0 us
  matrix products: 605 us -> 0 us
  Pallas kernels: 0 us -> 160 us
  starting transfers between devices: 29.2 us -> 0 us
  local copies, waits for them, and re-layouts: 30.5 us -> 6.2 us
    ppermute x20 -> x0, waiting for transfers between devices: 1400 us -> none  [the longest x16 1400 us: run_stage(): x_left = lax.ppermute(x_run[-1], 'row', fwd_perm)]
    dot_general x384 -> x0, matrix products: 605 us -> none  [the longest x192 387 us: row_step(): jnp.dot(d_i, t_i.astype(jnp.bfloat16), preferred_element_type=jnp.float32)]
    pallas_call x0 -> x1, Pallas kernels: none -> 160 us  [call(): pl.pallas_call(kernel, out_shape=jax.ShapeDtypeStruct((n_rows, size, cols...]
    ppermute x20 -> x0, starting transfers between devices: 29.2 us -> none  [the longest x16 20.5 us: run_stage(): x_left = lax.ppermute(x_run[-1], 'row', fwd_perm)]
  transfers between devices with their start and end apart: 20 -> 0, of which waited for: 17 -> 0; matrix products, arithmetic and copies ran while one was open for 0% -> 0% of each run, Pallas kernels for 0% -> 0%
where the time goes in v1:
time: 166 us
  Pallas kernels  160 us (96%)
  local copies, waits for them, and re-layouts  6.2 us (4%)
    pallas_call x1, Pallas kernels, call(): pl.pallas_call(kernel, out_shape=jax.ShapeDtypeStruct((n_rows, size, cols...  160 us
    unnamed x1, local copies, waits for them, and re-layouts  6.2 us

profile of v1, /device:TPU:31, one launch (start us, length us, event | category | flops | bytes accessed | tf_op | source)
XLA Modules:
  0.0 166.2 jit_solution(9691446996461659983)
XLA Ops:
  0.0 160.0 %shard_map.55 = f32[48,256,128]{2,1,0:T(8,128)} custom-call(bf16[48,256,256]{2,1,0:T(8,128)(2,1)} %d_hbm.1, bf16[48,256,256]{2,1,0:T(8,128)(2,1)} %l_hbm.1, bf16[48,256,256]{2,1,0:T(8,128)(2,1)} %u_hbm.1, f32[48,256,128]{2,1,0:T(8,128)} %f_hbm.1, f32[48,256,128]{2,1,0:T(8,128)} %x_hbm.1), custom_call_target="tpu_custom_call" | custom-call | tf_op jit(solution)/shard_map/pallas_call | solution.py:292
  160.0 6.2 %copy.7 = f32[48,256,128]{2,1,0:T(8,128)} copy(f32[48,256,128]{2,1,0:T(8,128)} %shard_map.55) | data formatting | bytes 12582912

commit v2 on v1

--- a/solution.py
+++ b/solution.py
@@ -11,12 +11,7 @@
 UNROLL = 10
 RING = 10
 MESH = pl.DeviceIdType.MESH
-ORDER = (1, 2, 3, 4)
 BF16, F32 = jnp.bfloat16, jnp.float32
-
-
-def n_ok(name, ring):
-    return ring or name != "x"
 
 
 def dot(a, b):
@@ -36,7 +31,7 @@
     ghost = len(chunks)
 
     def kernel(d_hbm, l_hbm, u_hbm, f_hbm, x_hbm, o_hbm,
-               l_all, d_all, u_all, f_raw, x_raw, f_all, x_all, l_ring, d_ring, u_ring, f_ring, out, now, recv, send,
+               l_all, d_all, u_all, f_raw, x_raw, f_all, x_all, l_ring, d_ring, u_ring, f_ring, out, hold, recv, send,
                sem_l, sem_d, sem_u, sem_f, sem_x, sem_o, sem_g, sem_s, sem_r):
         me = lax.axis_index("row")
         arrays = {"l": (l_hbm, l_all, sem_l), "d": (d_hbm, d_all, sem_d), "u": (u_hbm, u_all, sem_u),
@@ -127,38 +122,70 @@
             def mat(name, base, r):
                 return prep_to[name][slot(base, r)]
 
-            def period(x, p, base=None):
-                x = dict(x)
-                if base is None and p % 2 == 0 and p < 2 * SWEEPS and not ring:
-                    k = p // 2 + 1
-                    boundary(k - 1).wait_recv()
-                    x[k] = recv[k - 1]
-                new = {}
-                for k in ORDER:
-                    if not active(k, p):
-                        continue
-                    r = p - 2 * (k - 1)
-                    if k == 1:
-                        right = x_all[where(base, r + 1)]
-                    else:
-                        right = x[k - 1]
+            def period(live, p, base=None, preps=()):
+                x = {}
+
+                def get_x(k):
+                    if ("x", k) in live:
+                        val = live.pop(("x", k))
+                        x[k] = val.astype(BF16)
+                        if k == SWEEPS:
+                            out[where(base, p - LEAD)] = val.T
+                        if base is None and p - 1 - 2 * (k - 1) == last_row:
+                            send[k - 1] = x[k]
+
+                            @pl.when(me < n_dev - 1)
+                            def _():
+                                boundary(k - 1).start()
+                    elif base is None and p == 2 * (k - 1) and not ring:
+                        boundary(k - 1).wait_recv()
+                        x[k] = recv[k - 1]
+
+                def add(k, val):
+                    live["t", k] = live["t", k] + val if ("t", k) in live else val
+
+                def mul_l(k):
+                    if active(k, p) and not (ring and base is None and p == 2 * (k - 1)):
+                        add(k, dot(x[k], mat("l", base, p - 2 * (k - 1))))
+
+                def mul_u(k):
+                    if active(k, p):
+                        r = p - 2 * (k - 1)
+                        val = x[k - 1]
                         if base is None and r == last_row:
-                            right = jnp.where(me < n_dev - 1, right, jnp.zeros_like(right))
-                    s = dot(right, mat("u", base, r))
-                    if k in x:
-                        s = s + dot(x[k], mat("l", base, r))
-                    t = (prep_to["f"][slot(base, r)] - s).astype(BF16)
-                    val = dot(t, mat("d", base, r))
-                    new[k] = val.astype(BF16)
-                    if k == SWEEPS:
-                        out[where(base, r)] = val.T
-                    if base is None and r == last_row:
-                        send[k - 1] = new[k]
-
-                        @pl.when(me < n_dev - 1)
-                        def _():
-                            boundary(k - 1).start()
-                return new
+                            val = jnp.where(me < n_dev - 1, val, jnp.zeros_like(val))
+                        add(k, dot(val, mat("u", base, r)))
+
+                def mul_u1(s):
+                    if active(1, s):
+                        add(1, dot(x_all[where(base, s + 1)], mat("u", base, s)))
+
+                def mul_d(k, s):
+                    if ("t", k) in live:
+                        r = s - 2 * (k - 1)
+                        t = (prep_to["f"][slot(base, r)] - live.pop(("t", k))).astype(BF16)
+                        live["x", k] = dot(t, mat("d", base, r))
+
+                for name, r in preps:
+                    prep(name, base, r)
+                if ("t", 1) not in live:
+                    mul_u1(p)
+                get_x(1)
+                mul_l(1)
+                mul_d(3, p - 1)
+                mul_u(2)
+                get_x(2)
+                mul_l(2)
+                mul_u(3)
+                mul_d(4, p - 1)
+                mul_d(1, p)
+                mul_u1(p + 1)
+                get_x(3)
+                mul_l(3)
+                mul_d(2, p)
+                mul_u(4)
+                get_x(4)
+                mul_l(4)
 
             def step_preps(p):
                 return [(n, p + 1) for n in "ldf"] + [("u", p + 2), ("x", p + 3)]
@@ -203,21 +230,23 @@
                 for r in range(n_rows, n_rows + GHOST + 1):
                     prep("x", None, r)
 
-            def keep(x):
-                for k in x:
-                    now[k - 1] = x[k]
+            def keep(live):
+                for k in (1, 2):
+                    hold[k - 1] = live["x", k]
+                for k in (1, 3, 4):
+                    hold[1 + max(k - 1, 1)] = live["t", k]
 
             def load():
-                return {k: now[k - 1] for k in range(1, SWEEPS + 1)}
-
-            x = {}
+                live = {("x", k): hold[k - 1] for k in (1, 2)}
+                return {**live, **{("t", k): hold[1 + max(k - 1, 1)] for k in (1, 3, 4)}}
+
+            live = {}
             for p in range(LEAD):
-                for name, r in step_preps(p) if ring else ():
+                preps = step_preps(p) if ring else ()
+                for name, r in preps:
                     need(name, r)
-                    prep(name, None, r)
-                x = period(x, p)
-            keep(x)
-            out_copy(trips + 2, 0, 1).start()
+                period(live, p, None, preps)
+            keep(live)
 
             def trip(b, carry):
                 base = LEAD + UNROLL * b
@@ -234,29 +263,27 @@
                     def _():
                         for name in "ux":
                             ghost_wait(name)
-                x = load()
+                live = load()
                 for j in range(UNROLL):
                     p = LEAD + j
-                    for name, r in step_preps(p) if ring else ():
-                        prep(name, base, r)
-                    x = period(x, p, base)
-                keep(x)
-                out_copy(b, 1 + UNROLL * b, UNROLL).start()
+                    period(live, p, base, step_preps(p) if ring else ())
+                keep(live)
+                out_copy(b, UNROLL * b, UNROLL).start()
                 return carry
             lax.fori_loop(0, trips, trip, 0)
 
             for name in "ldf" if ring else "uldf":
                 ghost_wait(name)
+            live = load()
             if not ring:
                 prep("u", None, n_rows)
-            x = load()
-            for p in range(main_end, end - 1):
-                for name, r in step_preps(p):
-                    if n_rows <= r < n_rows + GHOST and (n_ok(name, ring)) or (ring and name == "x" and r == n_rows + GHOST):
-                        prep(name, None, r)
-                x = {**x, **period(x, p)}
-                if p == end - 3:
-                    out_copy(trips, 1 + UNROLL * trips, n_rows - UNROLL * trips - 2).start()
+            for p in range(main_end, end):
+                preps = [(n, r) for n, r in step_preps(p) if n_rows <= r < n_rows + GHOST and (n != "x" or ring)]
+                if ring and p + 3 == n_rows + GHOST:
+                    preps.append(("x", p + 3))
+                period(live, p, None, preps)
+                if p == end - 2:
+                    out_copy(trips, UNROLL * trips, n_rows - UNROLL * trips - 1).start()
             out_copy(trips + 1, last_row, 1).start()
 
         @pl.when(me == 0)
@@ -277,9 +304,8 @@
             for i, name in enumerate("xuldf"):
                 ghost_copy(i, name).wait_send()
         for b in range(trips):
-            out_copy(b, 1 + UNROLL * b, UNROLL).wait()
-        out_copy(trips, 1 + UNROLL * trips, n_rows - UNROLL * trips - 2).wait()
-        out_copy(trips + 2, 0, 1).wait()
+            out_copy(b, UNROLL * b, UNROLL).wait()
+        out_copy(trips, UNROLL * trips, n_rows - UNROLL * trips - 1).wait()
         out_copy(trips + 1, last_row, 1).wait()
 
     def call(d_inv, l_blk, u_blk, rhs_blk, x_init):
@@ -297,8 +323,8 @@
             scratch_shapes=[
                 mat(ext), mat(ext), mat(ext), vec(ext), vec(ext + 1), vec_t(ext, F32), vec_t(ext + 1, BF16),
                 mat(RING), mat(RING), mat(RING), vec_t(RING, F32),
-                vec(n_rows), vec_t(SWEEPS, BF16), vec_t(SWEEPS, BF16), vec_t(SWEEPS, BF16),
-                *[dma((ghost + 1,)) for _ in range(5)], dma((trips + 3,)), dma((5,)), dma((SWEEPS,)), dma((SWEEPS,)),
+                vec(n_rows), vec_t(5, F32), vec_t(SWEEPS, BF16), vec_t(SWEEPS, BF16),
+                *[dma((ghost + 1,)) for _ in range(5)], dma((trips + 2,)), dma((5,)), dma((SWEEPS,)), dma((SWEEPS,)),
             ],
             compiler_params=pltpu.CompilerParams(
                 collective_id=0, has_side_effects=True, vmem_limit_bytes=67_000_000),

time: 166 us -> 78.7 us (0.47)
  Pallas kernels: 160 us -> 72.3 us
    pallas_call x1, Pallas kernels: 160 us -> 72.3 us  [call(): pl.pallas_call(kernel, out_shape=jax.ShapeDtypeStruct((n_rows, size, cols...]
where the time goes in v2:
time: 78.7 us; the launch traced here: 78.5 us
  Pallas kernels  72.3 us (92%)
  local copies, waits for them, and re-layouts  6.2 us (8%)
    pallas_call x1, Pallas kernels, call(): pl.pallas_call(kernel, out_shape=jax.ShapeDtypeStruct((n_rows, size, cols...  72.3 us
    unnamed x1, local copies, waits for them, and re-layouts  6.2 us

profile of v2, /device:TPU:31, one launch (start us, length us, event | category | flops | bytes accessed | tf_op | source)
XLA Modules:
  0.0 78.5 jit_solution(40782410976115656)
XLA Ops:
  0.0 72.3 %shard_map.55 = f32[48,256,128]{2,1,0:T(8,128)} custom-call(bf16[48,256,256]{2,1,0:T(8,128)(2,1)} %d_hbm.1, bf16[48,256,256]{2,1,0:T(8,128)(2,1)} %l_hbm.1, bf16[48,256,256]{2,1,0:T(8,128)(2,1)} %u_hbm.1, f32[48,256,128]{2,1,0:T(8,128)} %f_hbm.1, f32[48,256,128]{2,1,0:T(8,128)} %x_hbm.1), custom_call_target="tpu_custom_call" | custom-call | tf_op jit(solution)/shard_map/pallas_call | solution.py:318
  72.3 6.2 %copy.7 = f32[48,256,128]{2,1,0:T(8,128)} copy(f32[48,256,128]{2,1,0:T(8,128)} %shard_map.55) | data formatting | bytes 12582912

commit v3 on v2

--- a/solution.py
+++ b/solution.py
@@ -30,9 +30,9 @@
     assert first + UNROLL * trips == n_rows and UNROLL % RING == 0
     ghost = len(chunks)
 
-    def kernel(d_hbm, l_hbm, u_hbm, f_hbm, x_hbm, o_hbm,
-               l_all, d_all, u_all, f_raw, x_raw, f_all, x_all, l_ring, d_ring, u_ring, f_ring, out, hold, recv, send,
-               sem_l, sem_d, sem_u, sem_f, sem_x, sem_o, sem_g, sem_s, sem_r):
+    def kernel(d_hbm, l_hbm, u_hbm, f_hbm, x_hbm, out,
+               l_all, d_all, u_all, f_raw, x_raw, f_all, x_all, l_ring, d_ring, u_ring, f_ring, hold, recv, send,
+               sem_l, sem_d, sem_u, sem_f, sem_x, sem_g, sem_s, sem_r):
         me = lax.axis_index("row")
         arrays = {"l": (l_hbm, l_all, sem_l), "d": (d_hbm, d_all, sem_d), "u": (u_hbm, u_all, sem_u),
                   "f": (f_hbm, f_raw, sem_f), "x": (x_hbm, x_raw, sem_x)}
@@ -92,10 +92,6 @@
             return pltpu.make_async_remote_copy(
                 src_ref=send.at[k], dst_ref=recv.at[k], send_sem=sem_s.at[k], recv_sem=sem_r.at[k],
                 device_id={"row": me + 1}, device_id_type=MESH)
-
-        def out_copy(i, start, size):
-            rows = pl.ds(start, size)
-            return pltpu.make_async_copy(out.at[rows], o_hbm.at[rows], sem_o.at[i])
 
         def run(ring):
             def where(base, p):
@@ -268,7 +264,6 @@
                     p = LEAD + j
                     period(live, p, base, step_preps(p) if ring else ())
                 keep(live)
-                out_copy(b, UNROLL * b, UNROLL).start()
                 return carry
             lax.fori_loop(0, trips, trip, 0)
 
@@ -282,9 +277,6 @@
                 if ring and p + 3 == n_rows + GHOST:
                     preps.append(("x", p + 3))
                 period(live, p, None, preps)
-                if p == end - 2:
-                    out_copy(trips, UNROLL * trips, n_rows - UNROLL * trips - 1).start()
-            out_copy(trips + 1, last_row, 1).start()
 
         @pl.when(me == 0)
         def _():
@@ -303,10 +295,6 @@
         def _():
             for i, name in enumerate("xuldf"):
                 ghost_copy(i, name).wait_send()
-        for b in range(trips):
-            out_copy(b, UNROLL * b, UNROLL).wait()
-        out_copy(trips, UNROLL * trips, n_rows - UNROLL * trips - 1).wait()
-        out_copy(trips + 1, last_row, 1).wait()
 
     def call(d_inv, l_blk, u_blk, rhs_blk, x_init):
         size = d_inv.shape[-1]
@@ -317,17 +305,17 @@
         vec = lambda n: pltpu.VMEM((n, size, cols), F32)
         return pl.pallas_call(
             kernel,
-            out_shape=jax.ShapeDtypeStruct((n_rows, size, cols), F32),
+            out_shape=pltpu.VMEM((n_rows, size, cols), F32),
             in_specs=[pl.BlockSpec(memory_space=pltpu.HBM)] * 5,
-            out_specs=pl.BlockSpec(memory_space=pltpu.HBM),
+            out_specs=pl.BlockSpec(memory_space=pltpu.VMEM),
             scratch_shapes=[
                 mat(ext), mat(ext), mat(ext), vec(ext), vec(ext + 1), vec_t(ext, F32), vec_t(ext + 1, BF16),
                 mat(RING), mat(RING), mat(RING), vec_t(RING, F32),
-                vec(n_rows), vec_t(5, F32), vec_t(SWEEPS, BF16), vec_t(SWEEPS, BF16),
-                *[dma((ghost + 1,)) for _ in range(5)], dma((trips + 2,)), dma((5,)), dma((SWEEPS,)), dma((SWEEPS,)),
+                vec_t(5, F32), vec_t(SWEEPS, BF16), vec_t(SWEEPS, BF16),
+                *[dma((ghost + 1,)) for _ in range(5)], dma((5,)), dma((SWEEPS,)), dma((SWEEPS,)),
             ],
             compiler_params=pltpu.CompilerParams(
-                collective_id=0, has_side_effects=True, vmem_limit_bytes=67_000_000),
+                collective_id=0, has_side_effects=True, vmem_limit_bytes=58_000_000),
         )(d_inv, l_blk, u_blk, rhs_blk, x_init)
 
     return call

time: 78.7 us -> 74.2 us (0.943)
  local copies, waits for them, and re-layouts: 6.2 us -> 2.71 us
  Pallas kernels: 72.3 us -> 71.4 us
    unnamed x1, local copies, waits for them, and re-layouts: 6.2 us -> 2.71 us
    pallas_call x1, Pallas kernels: 72.3 us -> 71.4 us  [call(): pl.pallas_call(kernel, out_shape=pltpu.VMEM((n_rows, size, cols), F32), i...]
where the time goes in v3:
time: 74.2 us; the launch traced here: 74.1 us
  Pallas kernels  71.4 us (96%)
  local copies, waits for them, and re-layouts  2.71 us (4%)
    pallas_call x1, Pallas kernels, call(): pl.pallas_call(kernel, out_shape=pltpu.VMEM((n_rows, size, cols), F32), i...  71.4 us
    unnamed x1, local copies, waits for them, and re-layouts  2.71 us

profile of v3, /device:TPU:31, one launch (start us, length us, event | category | flops | bytes accessed | tf_op | source)
XLA Modules:
  0.0 74.1 jit_solution(2416653247454932549)
XLA Ops:
  0.0 71.4 %shard_map.55 = f32[48,256,128]{2,1,0:T(8,128)S(1)} custom-call(bf16[48,256,256]{2,1,0:T(8,128)(2,1)} %d_hbm.1, bf16[48,256,256]{2,1,0:T(8,128)(2,1)} %l_hbm.1, bf16[48,256,256]{2,1,0:T(8,128)(2,1)} %u_hbm.1, f32[48,256,128]{2,1,0:T(8,128)} %f_hbm.1, f32[48,256,128]{2,1,0:T(8,128)} %x_hbm.1), custom_call_target="tpu_custom_call" | custom-call | tf_op jit(solution)/shard_map/pallas_call | solution.py:306
  71.4 2.7 %copy.7 = f32[48,256,128]{2,1,0:T(8,128)} copy(f32[48,256,128]{2,1,0:T(8,128)S(1)} %shard_map.55) | data formatting | bytes 12582912

commit v4 on v0

v4 whole, which is shorter than its diff:
```python
import jax
import jax.numpy as jnp
from jax import lax
from jax.experimental import pallas as pl
from jax.experimental.pallas import tpu as pltpu
from jax.sharding import PartitionSpec as P

SWEEPS = 4
GHOST = SWEEPS - 1
LEAD = 2 * SWEEPS - 1
LEAD_FIRST = LEAD + 10
TRIP_FIRST = 10
TRIP = 20
RING = 10
CHUNKS = (1, 1, 2, 4, 4, 6)
MESH = pl.DeviceIdType.MESH
BF16, F32 = jnp.bfloat16, jnp.float32
NAMES = "uxdfl"


def dot(a, b):
    return jnp.dot(a, b, preferred_element_type=F32)


def make_kernel(n_dev, n_rows, size, cols):
    last_row = n_rows - 1
    end = n_rows + LEAD
    sizes = list(CHUNKS) + [TRIP_FIRST] * ((n_rows - sum(CHUNKS)) // TRIP_FIRST)
    starts = [sum(sizes[:i]) for i in range(len(sizes))]
    assert sum(sizes) == n_rows and sum(CHUNKS) == LEAD_FIRST + 1 and TRIP_FIRST % RING == 0
    ghost = len(sizes)
    trips_first = ghost - len(CHUNKS)
    trips = (n_rows - 1 - LEAD) // TRIP

    def kernel(d_hbm, l_hbm, u_hbm, f_hbm, x_hbm, out,
               ul_all, d_all, f_raw, x_raw, f_all, x_all, ul_ring, d_ring, f_ring, hold, recv, send,
               sem_l, sem_d, sem_u, sem_f, sem_x, sem_g, sem_s, sem_r):
        me = lax.axis_index("row")
        hbm = {"l": l_hbm, "d": d_hbm, "u": u_hbm, "f": f_hbm, "x": x_hbm}
        sems = {"l": sem_l, "d": sem_d, "u": sem_u, "f": sem_f, "x": sem_x}
        half = {"u": pl.ds(0, size), "l": pl.ds(size, size)}

        def landing(name, rows):
            if name in half:
                return ul_all.at[rows, half[name]]
            return {"d": d_all, "f": f_raw, "x": x_raw}[name].at[rows]

        def local(name, c, start, n):
            if name == "x":
                start = start + 1
            rows = pl.ds(start, n)
            return pltpu.make_async_copy(hbm[name].at[rows], landing(name, rows), sems[name].at[c])

        def chunk(name, c):
            last = name == "x" and c == ghost - 1
            return local(name, c, starts[c], sizes[c] - last)

        for c in range(ghost):
            for name in NAMES:
                chunk(name, c).start()

        def ghost_rows(name):
            return GHOST + 1 if name == "x" else GHOST

        def ghost_copy(i, name):
            n = ghost_rows(name)
            return pltpu.make_async_remote_copy(
                src_ref=hbm[name].at[pl.ds(0, n)], dst_ref=landing(name, pl.ds(n_rows, n)), send_sem=sem_g.at[i],
                recv_sem=sems[name].at[ghost], device_id={"row": me - 1}, device_id_type=MESH)

        def ghost_local(name):
            n = ghost_rows(name)
            return pltpu.make_async_copy(
                hbm[name].at[pl.ds(0, n)], landing(name, pl.ds(n_rows, n)), sems[name].at[ghost])

        def ghost_wait(name):
            ghost_local(name).wait()

        barrier = pltpu.get_barrier_semaphore()

        @pl.when(me > 0)
        def _():
            pl.semaphore_signal(barrier, inc=1, device_id={"row": me - 1}, device_id_type=MESH)

        @pl.when(me < n_dev - 1)
        def _():
            pl.semaphore_signal(barrier, inc=1, device_id={"row": me + 1}, device_id_type=MESH)

        pl.semaphore_wait(barrier, jnp.where(me > 0, 1, 0) + jnp.where(me < n_dev - 1, 1, 0))

        @pl.when(me > 0)
        def _():
            for i, name in enumerate("xuldf"):
                ghost_copy(i, name).start()

        @pl.when(me == n_dev - 1)
        def _():
            for name in "xuldf":
                ghost_local(name).start()

        def boundary(k):
            return pltpu.make_async_remote_copy(
                src_ref=send.at[k], dst_ref=recv.at[k], send_sem=sem_s.at[k], recv_sem=sem_r.at[k],
                device_id={"row": me + 1}, device_id_type=MESH)

        def run(ring):
            lead = LEAD_FIRST if ring else LEAD
            per_trip, n_trips = (TRIP_FIRST, trips_first) if ring else (TRIP, trips)
            main_end = lead + per_trip * n_trips
            ul, d, f = (ul_ring, d_ring, f_ring) if ring else (ul_all, d_all, f_all)

            def where(base, p):
                return p if base is None else base + (p - lead)

            def slot(base, r):
                return r % RING if ring else where(base, r)

            def prep(base, r):
                at, to = where(base, r), slot(base, r)
                for name in "ul":
                    ul[to, half[name]] = ul_all[at, half[name]].T
                d[to] = d_all[at].T
                f[to] = f_raw[at].T
                x_all[at + 1] = x_raw[at + 1].astype(BF16).T

            def active(k, s):
                return 0 <= s - 2 * (k - 1) <= last_row + SWEEPS - k

            def period(live, p, base=None):
                x = {}

                def get_x(k):
                    if ("x", k) in live:
                        val = live.pop(("x", k))
                        x[k] = val.astype(BF16)
                        if k == SWEEPS:
                            out[where(base, p - LEAD)] = val.T
                        if base is None and p - 1 - 2 * (k - 1) == last_row:
                            send[k - 1] = x[k]

                            @pl.when(me < n_dev - 1)
                            def _():
                                boundary(k - 1).start()
                    elif base is None and p == 2 * (k - 1) and not ring:
                        boundary(k - 1).wait_recv()
                        x[k] = recv[k - 1]

                def sums(k):
                    get_x(k)
                    if not active(k, p):
                        return
                    r = p - 2 * (k - 1)
                    right = x_all[where(base, r + 1)] if k == 1 else x[k - 1]
                    if base is None and k > 1 and r == last_row:
                        right = jnp.where(me < n_dev - 1, right, jnp.zeros_like(right))
                    if k in x:
                        live["t", k] = dot(jnp.concatenate([right, x[k]], axis=1), ul[slot(base, r)])
                    else:
                        live["t", k] = dot(right, ul[slot(base, r), half["u"]])

                def solve(k, s):
                    if ("t", k) in live:
                        to = slot(base, s - 2 * (k - 1))
                        live["x", k] = dot((f[to] - live.pop(("t", k))).astype(BF16), d[to])

                sums(1)
                sums(2)
                solve(3, p - 1)
                sums(3)
                solve(4, p - 1)
                solve(1, p)
                sums(4)
                solve(2, p)

            carried = (("x", 1), ("x", 2), ("t", 3), ("t", 4))

            def keep(live):
                for i, key in enumerate(carried):
                    hold[i] = live[key]

            def load():
                return {key: hold[i] for i, key in enumerate(carried)}

            if ring:
                waited = set()

                def need(r):
                    c = max(i for i, start in enumerate(starts) if start <= r)
                    if c not in waited:
                        waited.add(c)
                        for name in NAMES:
                            chunk(name, c).wait()

                need(0)
                prep(None, 0)
            else:
                for c in range(1, ghost):
                    for i in ([0, 1] if c == 1 else [c]):
                        for name in NAMES:
                            chunk(name, i).wait()
                    if c == ghost - 1:
                        ghost_wait("x")
                    start = 0 if c == 1 else starts[c]

                    def pair(i, carry, start=start):
                        prep(start + 2 * i, lead)
                        prep(start + 2 * i, lead + 1)
                        return carry
                    lax.fori_loop(0, (starts[c] + sizes[c] - start) // 2, pair, 0)
            live = {}
            for p in range(lead):
                if ring:
                    need(p + 1)
                    prep(None, p + 1)
                period(live, p)
            keep(live)

            def trip(b, carry):
                base = lead + per_trip * b
                if ring:
                    c, start = len(CHUNKS) + b, lead + 1 + per_trip * b
                    for name in "udfl":
                        local(name, c, start, per_trip).wait()

                    @pl.when(b < n_trips - 1)
                    def _():
                        local("x", c, start, per_trip).wait()

                    @pl.when(b == n_trips - 1)
                    def _():
                        chunk("x", ghost - 1).wait()
                        ghost_wait("x")
                live = load()
                for p in range(lead, lead + per_trip):
                    if ring:
                        prep(base, p + 1)
                    period(live, p, base)
                keep(live)
                return carry
            lax.fori_loop(0, n_trips, trip, 0)

            for name in "uldf":
                ghost_wait(name)
            live = load()
            for p in range(main_end, end):
                if n_rows <= p + 1 < n_rows + GHOST:
                    prep(None, p + 1)
                period(live, p)

        @pl.when(me == 0)
        def _():
            run(True)

        @pl.when(me > 0)
        def _():
            run(False)

        @pl.when(me < n_dev - 1)
        def _():
            for k in range(SWEEPS):
                boundary(k).wait_send()

        @pl.when(me > 0)
        def _():
            for i, name in enumerate("xuldf"):
                ghost_copy(i, name).wait_send()

    ext = n_rows + GHOST
    dma = pltpu.SemaphoreType.DMA

    def vmem(dtype, *shape):
        return pltpu.VMEM(shape, dtype)

    return pl.pallas_call(
        kernel,
        out_shape=pltpu.VMEM((n_rows, size, cols), F32),
        in_specs=[pl.BlockSpec(memory_space=pltpu.HBM)] * 5,
        out_specs=pl.BlockSpec(memory_space=pltpu.VMEM),
        scratch_shapes=[
            vmem(BF16, ext, 2 * size, size), vmem(BF16, ext, size, size),
            vmem(F32, ext, size, cols), vmem(F32, ext + 1, size, cols),
            vmem(F32, ext, cols, size), vmem(BF16, ext + 1, cols, size),
            vmem(BF16, RING, 2 * size, size), vmem(BF16, RING, size, size), vmem(F32, RING, cols, size),
            vmem(F32, 4, cols, size), vmem(BF16, SWEEPS, cols, size), vmem(BF16, SWEEPS, cols, size),
            *[dma((ghost + 1,)) for _ in range(5)], dma((5,)), dma((SWEEPS,)), dma((SWEEPS,)),
        ],
        compiler_params=pltpu.CompilerParams(collective_id=0, has_side_effects=True, vmem_limit_bytes=58_000_000),
    )


def solution(mesh):
    mat_spec = P(("batch", "row"), None, None)
    vec_spec = P(("batch", "row"), None, "col")
    n_dev = mesh.shape["row"]

    def device_fn(d_inv, l_blk, u_blk, rhs_blk, x_init):
        return make_kernel(n_dev, *rhs_blk.shape)(d_inv, l_blk, u_blk, rhs_blk, x_init)

    return jax.shard_map(device_fn, mesh=mesh, in_specs=(mat_spec, mat_spec, mat_spec, vec_spec, vec_spec), out_specs=vec_spec, check_vma=False)
```

time: 2080 us -> 65.8 us (0.03)
  waiting for transfers between devices: 1400 us -> 0 us
  matrix products: 605 us -> 0 us
  Pallas kernels: 0 us -> 63 us
  starting transfers between devices: 29.2 us -> 0 us
  local copies, waits for them, and re-layouts: 30.5 us -> 2.71 us
    ppermute x20 -> x0, waiting for transfers between devices: 1400 us -> none  [the longest x16 1400 us: run_stage(): x_left = lax.ppermute(x_run[-1], 'row', fwd_perm)]
    dot_general x384 -> x0, matrix products: 605 us -> none  [the longest x192 387 us: row_step(): jnp.dot(d_i, t_i.astype(jnp.bfloat16), preferred_element_type=jnp.float32)]
    pallas_call x0 -> x1, Pallas kernels: none -> 63 us  [device_fn(): make_kernel(n_dev, *rhs_blk.shape)(d_inv, l_blk, u_blk, rhs_blk, x_init)]
    ppermute x20 -> x0, starting transfers between devices: 29.2 us -> none  [the longest x16 20.5 us: run_stage(): x_left = lax.ppermute(x_run[-1], 'row', fwd_perm)]
  transfers between devices with their start and end apart: 20 -> 0, of which waited for: 17 -> 0; matrix products, arithmetic and copies ran while one was open for 0% -> 0% of each run, Pallas kernels for 0% -> 0%
where the time goes in v4:
time: 65.8 us; the launch traced here: 65.7 us
  Pallas kernels  63 us (96%)
  local copies, waits for them, and re-layouts  2.71 us (4%)
    pallas_call x1, Pallas kernels, device_fn(): make_kernel(n_dev, *rhs_blk.shape)(d_inv, l_blk, u_blk, rhs_blk, x_init)  63 us
    unnamed x1, local copies, waits for them, and re-layouts  2.71 us

profile of v4, /device:TPU:31, one launch (start us, length us, event | category | flops | bytes accessed | tf_op | source)
XLA Modules:
  0.0 65.7 jit_solution(4129942434071145897)
XLA Ops:
  0.0 63.0 %shard_map.55 = f32[48,256,128]{2,1,0:T(8,128)S(1)} custom-call(bf16[48,256,256]{2,1,0:T(8,128)(2,1)} %d_hbm.1, bf16[48,256,256]{2,1,0:T(8,128)(2,1)} %l_hbm.1, bf16[48,256,256]{2,1,0:T(8,128)(2,1)} %u_hbm.1, f32[48,256,128]{2,1,0:T(8,128)} %f_hbm.1, f32[48,256,128]{2,1,0:T(8,128)} %x_hbm.1), custom_call_target="tpu_custom_call" | custom-call | tf_op jit(solution)/shard_map/pallas_call | solution.py:297
  63.0 2.7 %copy.7 = f32[48,256,128]{2,1,0:T(8,128)} copy(f32[48,256,128]{2,1,0:T(8,128)S(1)} %shard_map.55) | data formatting | bytes 12582912

commit v5 on v4

--- a/solution.py
+++ b/solution.py
@@ -10,9 +10,10 @@
 LEAD = 2 * SWEEPS - 1
 LEAD_FIRST = LEAD + 10
 TRIP_FIRST = 10
-TRIP = 20
+TRIP = 40
 RING = 10
 CHUNKS = (1, 1, 2, 4, 4, 6)
+EARLY = 4
 MESH = pl.DeviceIdType.MESH
 BF16, F32 = jnp.bfloat16, jnp.float32
 NAMES = "uxdfl"
@@ -55,9 +56,15 @@
             last = name == "x" and c == ghost - 1
             return local(name, c, starts[c], sizes[c] - last)
 
-        for c in range(ghost):
+        for c in range(EARLY):
             for name in NAMES:
                 chunk(name, c).start()
+
+        @pl.when(me > 0)
+        def _():
+            for c in range(EARLY, ghost):
+                for name in NAMES:
+                    chunk(name, c).start()
 
         def ghost_rows(name):
             return GHOST + 1 if name == "x" else GHOST
@@ -115,25 +122,39 @@
             def slot(base, r):
                 return r % RING if ring else where(base, r)
 
+            def prep_one(name, base, r):
+                at, to = where(base, r), slot(base, r)
+                if name in half:
+                    ul[to, half[name]] = ul_all[at, half[name]].T
+                elif name == "d":
+                    d[to] = d_all[at].T
+                elif name == "f":
+                    f[to] = f_raw[at].T
+                else:
+                    x_all[at + 1] = x_raw[at + 1].astype(BF16).T
+
             def prep(base, r):
-                at, to = where(base, r), slot(base, r)
-                for name in "ul":
-                    ul[to, half[name]] = ul_all[at, half[name]].T
-                d[to] = d_all[at].T
-                f[to] = f_raw[at].T
-                x_all[at + 1] = x_raw[at + 1].astype(BF16).T
+                for name in "uldfx":
+                    prep_one(name, base, r)
 
             def active(k, s):
                 return 0 <= s - 2 * (k - 1) <= last_row + SWEEPS - k
 
-            def period(live, p, base=None):
+            def period(live, p, base=None, row=None):
                 x = {}
+                left = [] if row is None else list("uldxf")
+
+                def fill():
+                    if left:
+                        prep_one(left.pop(0), base, row)
 
                 def get_x(k):
                     if ("x", k) in live:
                         val = live.pop(("x", k))
                         x[k] = val.astype(BF16)
-                        if k == SWEEPS:
+                        if k == SWEEPS and ring:
+                            f_all[where(base, p - LEAD)] = val
+                        elif k == SWEEPS:
                             out[where(base, p - LEAD)] = val.T
                         if base is None and p - 1 - 2 * (k - 1) == last_row:
                             send[k - 1] = x[k]
@@ -163,14 +184,19 @@
                         to = slot(base, s - 2 * (k - 1))
                         live["x", k] = dot((f[to] - live.pop(("t", k))).astype(BF16), d[to])
 
+                fill()
                 sums(1)
                 sums(2)
+                fill()
                 solve(3, p - 1)
                 sums(3)
+                fill()
                 solve(4, p - 1)
                 solve(1, p)
+                fill()
                 sums(4)
                 solve(2, p)
+                fill()
 
             carried = (("x", 1), ("x", 2), ("t", 3), ("t", 4))
 
@@ -209,10 +235,12 @@
                     lax.fori_loop(0, (starts[c] + sizes[c] - start) // 2, pair, 0)
             live = {}
             for p in range(lead):
+                if ring and p % 2 and EARLY + p // 2 < ghost:
+                    for name in NAMES:
+                        chunk(name, EARLY + p // 2).start()
                 if ring:
                     need(p + 1)
-                    prep(None, p + 1)
-                period(live, p)
+                period(live, p, None, p + 1 if ring else None)
             keep(live)
 
             def trip(b, carry):
@@ -232,9 +260,7 @@
                         ghost_wait("x")
                 live = load()
                 for p in range(lead, lead + per_trip):
-                    if ring:
-                        prep(base, p + 1)
-                    period(live, p, base)
+                    period(live, p, base, p + 1 if ring else None)
                 keep(live)
                 return carry
             lax.fori_loop(0, n_trips, trip, 0)
@@ -243,9 +269,13 @@
                 ghost_wait(name)
             live = load()
             for p in range(main_end, end):
-                if n_rows <= p + 1 < n_rows + GHOST:
-                    prep(None, p + 1)
-                period(live, p)
+                period(live, p, None, p + 1 if n_rows <= p + 1 < n_rows + GHOST else None)
+            if ring:
+                def turn(i, carry):
+                    for j in range(2):
+                        out[2 * i + j] = f_all[2 * i + j].T
+                    return carry
+                lax.fori_loop(0, n_rows // 2, turn, 0)
 
         @pl.when(me == 0)
         def _():

time: 65.8 us -> 64.1 us (0.974)
  Pallas kernels: 63 us -> 61.3 us
    pallas_call x1, Pallas kernels: 63 us -> 61.3 us  [device_fn(): make_kernel(n_dev, *rhs_blk.shape)(d_inv, l_blk, u_blk, rhs_blk, x_init)]
where the time goes in v5:
time: 64.1 us; the launch traced here: 64 us
  Pallas kernels  61.3 us (96%)
  local copies, waits for them, and re-layouts  2.71 us (4%)
    pallas_call x1, Pallas kernels, device_fn(): make_kernel(n_dev, *rhs_blk.shape)(d_inv, l_blk, u_blk, rhs_blk, x_init)  61.3 us
    unnamed x1, local copies, waits for them, and re-layouts  2.71 us

profile of v5, /device:TPU:31, one launch (start us, length us, event | category | flops | bytes accessed | tf_op | source)
XLA Modules:
  0.0 64.0 jit_solution(4310802020776226188)
XLA Ops:
  0.0 61.3 %shard_map.55 = f32[48,256,128]{2,1,0:T(8,128)S(1)} custom-call(bf16[48,256,256]{2,1,0:T(8,128)(2,1)} %d_hbm.1, bf16[48,256,256]{2,1,0:T(8,128)(2,1)} %l_hbm.1, bf16[48,256,256]{2,1,0:T(8,128)(2,1)} %u_hbm.1, f32[48,256,128]{2,1,0:T(8,128)} %f_hbm.1, f32[48,256,128]{2,1,0:T(8,128)} %x_hbm.1), custom_call_target="tpu_custom_call" | custom-call | tf_op jit(solution)/shard_map/pallas_call | solution.py:327
  61.3 2.7 %copy.7 = f32[48,256,128]{2,1,0:T(8,128)} copy(f32[48,256,128]{2,1,0:T(8,128)S(1)} %shard_map.55) | data formatting | bytes 12582912

commit v6 on v5

--- a/solution.py
+++ b/solution.py
@@ -185,10 +185,10 @@
                         live["x", k] = dot((f[to] - live.pop(("t", k))).astype(BF16), d[to])
 
                 fill()
+                solve(3, p - 1)
                 sums(1)
                 sums(2)
                 fill()
-                solve(3, p - 1)
                 sums(3)
                 fill()
                 solve(4, p - 1)
@@ -241,8 +241,6 @@
                 if ring:
                     need(p + 1)
                 period(live, p, None, p + 1 if ring else None)
-            keep(live)
-
             def trip(b, carry):
                 base = lead + per_trip * b
                 if ring:
@@ -263,11 +261,16 @@
                     period(live, p, base, p + 1 if ring else None)
                 keep(live)
                 return carry
-            lax.fori_loop(0, n_trips, trip, 0)
+            if ring:
+                keep(live)
+                lax.fori_loop(0, n_trips, trip, 0)
+                live = load()
+            else:
+                for p in range(lead, main_end):
+                    period(live, p)
 
             for name in "uldf":
                 ghost_wait(name)
-            live = load()
             for p in range(main_end, end):
                 period(live, p, None, p + 1 if n_rows <= p + 1 < n_rows + GHOST else None)
             if ring:

time: 64.1 us -> 64 us (level)
  no operation moved by 1% of the time
where the time goes in v6:
time: 64 us; the launch traced here: 63.9 us
  Pallas kernels  61.1 us (95%)
  local copies, waits for them, and re-layouts  2.71 us (4%)
    pallas_call x1, Pallas kernels, device_fn(): make_kernel(n_dev, *rhs_blk.shape)(d_inv, l_blk, u_blk, rhs_blk, x_init)  61.1 us
    unnamed x1, local copies, waits for them, and re-layouts  2.71 us

profile of v6, /device:TPU:31, one launch (start us, length us, event | category | flops | bytes accessed | tf_op | source)
XLA Modules:
  0.0 63.9 jit_solution(17971694368471563008)
XLA Ops:
  0.0 61.1 %shard_map.55 = f32[48,256,128]{2,1,0:T(8,128)S(1)} custom-call(bf16[48,256,256]{2,1,0:T(8,128)(2,1)} %d_hbm.1, bf16[48,256,256]{2,1,0:T(8,128)(2,1)} %l_hbm.1, bf16[48,256,256]{2,1,0:T(8,128)(2,1)} %u_hbm.1, f32[48,256,128]{2,1,0:T(8,128)} %f_hbm.1, f32[48,256,128]{2,1,0:T(8,128)} %x_hbm.1), custom_call_target="tpu_custom_call" | custom-call | tf_op jit(solution)/shard_map/pallas_call | solution.py:330
  61.2 2.7 %copy.7 = f32[48,256,128]{2,1,0:T(8,128)} copy(f32[48,256,128]{2,1,0:T(8,128)S(1)} %shard_map.55) | data formatting | bytes 12582912
